TPU v7x, 32 devices: a whole 2x2x4 slice. The times are simulated.
32 devices in a mesh: section: 8 (over z, y), dp: 4 (over x, core).
Axes of the slice: x: 2, y: 2, z: 4, core: 2. Of those that a mesh axis runs over, the one named last changes fastest.
Arguments:
- vit_weight: bfloat16 [8, 1280, 1280], P('section', 'dp'), may hold values from -0.078125 to 0.078125
- t5_weight: bfloat16 [8, 2048, 2048], P('section', 'dp'), may hold values from -0.0625 to 0.0625
- vit_saved: bfloat16 [8, 4, 128, 1280], P('section', None, 'dp'), may hold values from -6 to 6
- t5_saved: bfloat16 [8, 4, 128, 2048], P('section', None, 'dp'), may hold values from -6 to 6
- vit_top_grad: bfloat16 [4, 128, 1280], P(None, 'dp'), may hold values from -6 to 6
- t5_top_grad: bfloat16 [4, 128, 2048], P(None, 'dp'), may hold values from -6 to 6
Outputs:
- vit_input_grads: bfloat16 [8, 4, 128, 1280], P('section', None, 'dp')
- t5_input_grads: bfloat16 [8, 4, 128, 2048], P('section', None, 'dp')
- vit_weight_grads: float32 [8, 1280, 1280], P('section', 'dp')
- t5_weight_grads: float32 [8, 2048, 2048], P('section', 'dp')
All inputs are finite; a program needn't handle non-finite values.
Results may differ from a plain program's by a relative error of at most 0.02.
Values may be sent and summed in bfloat16 or wider, within the bound.
A program may use at most 128 MiB of HBM per device.

v0:
```python
import functools

import jax
import jax.numpy as jnp
from jax import lax
from jax.experimental import pallas as pl
from jax.experimental.pallas import tpu as pltpu
from jax.sharding import PartitionSpec as P

root_half = 0.7071067811865476
inv_root_tau = 0.3989422804014327
MESH = pl.DeviceIdType.MESH


def gelu_slope(preact):
    cumulative = 0.5 * (1.0 + lax.erf(preact * root_half))
    density = jnp.exp(-0.5 * preact * preact) * inv_root_tau
    return cumulative + preact * density


class Branch:
    def __init__(self, ins, outs, scratch):
        self.weight_in, self.saved_in, self.top_in = ins
        self.out, self.columns, self.local = outs
        (
            self.weight,
            self.saved,
            self.top,
            self.above,
            self.lifted,
            self.lift_sem,
            self.below,
            self.mine,
            self.pair_out,
            self.pair_in,
            self.chip_in,
            self.slope,
            self.saved_sem,
            self.top_sem,
            self.pair_sem,
            self.chip_sem,
            self.near_sem,
            self.far_sem,
            self.hop_sem,
            self.out_sem,
        ) = scratch


BRANCH_SCRATCH = 20


def kernel(sections, parts, micros, *refs):
    ins, outs, scratch = refs[:6], refs[6:12], refs[12:]
    branches = [
        Branch(ins[3 * b : 3 * b + 3], outs[3 * b : 3 * b + 3],
               scratch[BRANCH_SCRATCH * b : BRANCH_SCRATCH * (b + 1)])
        for b in range(2)
    ]
    section = lax.axis_index("section")
    me = lax.axis_index("dp")
    chips = parts // 2
    chip, core = me // 2, me % 2
    partner = chip * 2 + 1 - core
    is_last = section == sections - 1
    is_first = section == 0

    def ahead(k):
        return lax.rem(chip + k, chips) * 2 + core

    def behind(k):
        return lax.rem(chip + chips - k, chips) * 2 + core

    def other(group):
        return group + 1 - 2 * core

    def copy(src, dst, sems, index, where, part):
        return pltpu.make_async_remote_copy(
            src_ref=src, dst_ref=dst, send_sem=sems.at[(0, *index)], recv_sem=sems.at[(1, *index)],
            device_id=(where, part), device_id_type=MESH,
        )

    def regroup(source, groups):
        size = groups.shape[-1]
        for group in range(parts):
            groups[group] = source[..., group * size : (group + 1) * size]

    barrier = pltpu.get_barrier_semaphore()
    for k in range(1, parts):
        pl.semaphore_signal(barrier, inc=1, device_id=(section, lax.rem(me + k, parts)), device_id_type=MESH)

    def greet(other_section):
        pl.semaphore_signal(barrier, inc=1, device_id=(other_section, me), device_id_type=MESH)

    @pl.when(is_last)
    def _():
        pl.loop(0, sections - 1)(greet)

    @pl.when(jnp.logical_not(is_last))
    def _():
        greet(sections - 1)

        @pl.when(section > 0)
        def _():
            greet(section - 1)

        @pl.when(section < sections - 2)
        def _():
            greet(section + 1)

    for br in branches:
        regroup(br.saved_in, br.saved)
    below_last = lax.min(sections - 1 - section, 1)
    column = below_last * (1 + lax.min(section, 1) + lax.min(lax.max(sections - 2 - section, 0), 1))
    pl.semaphore_wait(barrier, parts - 1 + column + (1 - below_last) * (sections - 1))

    def saved_copy(br, m, k):
        to = lax.rem(me + k, parts)
        return copy(br.saved.at[to, m], br.columns.at[m, me], br.saved_sem, (m, k - 1), section, to)

    def top_copy(br, m, k):
        to = lax.rem(me + k, parts)
        return copy(br.top.at[to, m], br.lifted.at[m, me], br.top_sem, (m, k - 1), section, to)

    def lift_copy(br, m):
        return copy(br.lifted.at[m], br.above.at[m], br.lift_sem, (m,), sections - 1, me)

    def helper(m):
        return sections - 1 - lax.rem(m, sections)

    def pair_copy(br, m):
        return copy(br.pair_out.at[m], br.pair_in.at[m], br.pair_sem, (m,), section, partner)

    def chip_copy(br, m, k):
        return copy(br.mine.at[m, k], br.chip_in.at[m, k - 1], br.chip_sem, (m, k - 1), section, ahead(k))

    def near_copy(br, m, k):
        group = behind(k)
        return copy(br.local.at[m, group], br.local.at[m, group], br.near_sem, (m, k), section, partner)

    def far_copy(br, m, k):
        return copy(br.local.at[m, me], br.local.at[m, me], br.far_sem, (m, k - 1), section, ahead(k))

    def hop_copy(br, m):
        return copy(br.below.at[m], br.above.at[m], br.hop_sem, (m,), lax.max(section - 1, 0), me)

    def out_copy(br, m, k):
        to = lax.rem(me + k, parts)
        return copy(br.below.at[m, to], br.out.at[me, m], br.out_sem, (m, k - 1), section, to)

    def rows(block):
        return block.reshape(-1, block.shape[-1])

    def send_saved(m):
        for br in branches:
            for k in range(1, parts):
                saved_copy(br, m, k).start()

    def send_top(m):
        for br in branches:
            for k in range(1, parts):
                top_copy(br, m, k).start()

    def partial(half):
        size = micros // 2
        first = half * size

        @pl.loop(first, first + size)
        def _(m):
            for br in branches:
                br.columns[m, me] = br.saved[me, m]
                for k in range(1, parts):
                    saved_copy(br, m, k).wait_recv()

        span = pl.ds(first, size)
        for br in branches:
            tokens = rows(br.columns[span])

            def product(group):
                block = jnp.dot(tokens, br.weight[group], preferred_element_type=jnp.float32)
                return block.astype(jnp.bfloat16).reshape(size, -1, block.shape[-1])

            for k in range(chips):
                br.pair_out[span, k] = product(other(ahead(k)))

            @pl.loop(first, first + size)
            def _(m):
                pair_copy(br, m).start()

            for k in range(chips):
                br.mine[span, k] = product(ahead(k))

    def pair_sum(m):
        for br in branches:
            pair_copy(br, m).wait_recv()
            for k in range(1, chips):
                both = br.mine[m, k].astype(jnp.float32) + br.pair_in[m, k].astype(jnp.float32)
                br.mine[m, k] = both.astype(jnp.bfloat16)
                chip_copy(br, m, k).start()

    def find_slope(br, m):
        total = br.mine[m, 0].astype(jnp.float32) + br.pair_in[m, 0].astype(jnp.float32)
        for k in range(1, chips):
            chip_copy(br, m, k).wait_recv()
            total = total + br.chip_in[m, k - 1].astype(jnp.float32)
        br.slope[m] = gelu_slope(total)

    def gather_top(br, m):
        br.lifted[m, me] = br.top[me, m]
        for k in range(1, parts):
            top_copy(br, m, k).wait_recv()

    def spread(m):
        for br in branches:
            @pl.when(is_last)
            def _():
                find_slope(br, m)

                @pl.when(helper(m) == section)
                def _():
                    gather_top(br, m)
                    br.above[m] = br.lifted[m]

                @pl.when(helper(m) != section)
                def _():
                    lift_copy(br, m).wait_recv()

            @pl.when(jnp.logical_not(is_last))
            def _():
                hop_copy(br, m).wait_recv()

            br.local[m, me] = (rows(br.above[m]).astype(jnp.float32) * br.slope[m]).astype(jnp.bfloat16)
            for k in range(1, chips):
                far_copy(br, m, k).start()
            near_copy(br, m, 0).start()

    def descend(m):
        for br in branches:
            def through(group):
                return lax.dot_general(
                    br.local[m, group], br.weight[group], (((1,), (1,)), ((), ())),
                    preferred_element_type=jnp.float32,
                )

            for k in range(1, chips):
                far_copy(br, m, k).wait_recv()
                near_copy(br, m, k).start()
            total = rows(br.above[m]).astype(jnp.float32) + through(me)
            near_copy(br, m, 0).wait_recv()
            total = total + through(partner)
            for k in range(1, chips):
                total = total + through(behind(k))
            for k in range(1, chips):
                near_copy(br, m, k).wait_recv()
                total = total + through(other(behind(k)))
            br.below[m] = total.astype(jnp.bfloat16).reshape(br.below.shape[1:])

            @pl.when(jnp.logical_not(is_first))
            def _():
                hop_copy(br, m).start()

    def hand_out(m):
        for br in branches:
            br.out[me, m] = br.below[m, me]
            for k in range(1, parts):
                out_copy(br, m, k).start()

    ready = min(2, micros)
    pl.loop(0, micros)(send_saved)

    for br in branches:
        regroup(br.top_in, br.top)

    @pl.loop(0, micros)
    def _(m):
        @pl.when(helper(m) == section)
        def _():
            send_top(m)

    for br in branches:
        regroup(br.weight_in, br.weight)

    pl.loop(0, 2)(partial)

    @pl.when(is_last)
    def _():
        pl.loop(0, ready)(pair_sum)

    @pl.when(jnp.logical_not(is_last))
    def _():
        @pl.loop(0, micros)
        def _(m):
            @pl.when(helper(m) == section)
            def _():
                for br in branches:
                    gather_top(br, m)
                    lift_copy(br, m).start()

        pl.loop(0, micros)(pair_sum)

        @pl.loop(0, micros)
        def _(m):
            for br in branches:
                find_slope(br, m)

    @pl.loop(0, micros + 1)
    def _(step):
        @pl.when(step < micros)
        def _():
            spread(step)

        @pl.when(jnp.logical_and(is_last, step < micros - ready))
        def _():
            pair_sum(step + ready)

        @pl.when(step > 0)
        def _():
            descend(step - 1)

        @pl.when(jnp.logical_and(section < 2, step > 0))
        def _():
            hand_out(step - 1)

    @pl.when(section >= 2)
    def _():
        pl.loop(0, micros)(hand_out)

    @pl.loop(0, micros)
    def _(m):
        for br in branches:
            for k in range(1, parts):
                saved_copy(br, m, k).wait_send()
                out_copy(br, m, k).wait_send()
                out_copy(br, m, k).wait_recv()

            @pl.when(helper(m) == section)
            def _():
                for k in range(1, parts):
                    top_copy(br, m, k).wait_send()

                @pl.when(jnp.logical_not(is_last))
                def _():
                    lift_copy(br, m).wait_send()

            @pl.when(jnp.logical_not(is_first))
            def _():
                hop_copy(br, m).wait_send()

            pair_copy(br, m).wait_send()
            near_copy(br, m, 0).wait_send()
            for k in range(1, chips):
                chip_copy(br, m, k).wait_send()
                far_copy(br, m, k).wait_send()
                near_copy(br, m, k).wait_send()


def branch_call(sections, weights, saveds, tops):
    operands, outs, scratch = [], [], []
    for weight, saved, top in zip(weights, saveds, tops):
        rows, width = weight.shape
        micros, tokens = saved.shape[:2]
        parts = width // rows
        chips = parts // 2
        everyone = parts * tokens
        operands += [weight, saved, top]
        outs += [
            jax.ShapeDtypeStruct((parts, micros, tokens, rows), jnp.bfloat16),
            jax.ShapeDtypeStruct((micros, parts, tokens, rows), jnp.bfloat16),
            jax.ShapeDtypeStruct((micros, parts, everyone, rows), jnp.bfloat16),
        ]
        dma = pltpu.SemaphoreType.DMA
        scratch += [
            pltpu.VMEM((parts, rows, rows), jnp.bfloat16),
            pltpu.VMEM((parts, micros, tokens, rows), jnp.bfloat16),
            pltpu.VMEM((parts, micros, tokens, rows), jnp.bfloat16),
            pltpu.VMEM((micros, parts, tokens, rows), jnp.bfloat16),
            pltpu.VMEM((micros, parts, tokens, rows), jnp.bfloat16),
            dma((2, micros)),
            pltpu.VMEM((micros, parts, tokens, rows), jnp.bfloat16),
            pltpu.VMEM((micros, chips, everyone, rows), jnp.bfloat16),
            pltpu.VMEM((micros, chips, everyone, rows), jnp.bfloat16),
            pltpu.VMEM((micros, chips, everyone, rows), jnp.bfloat16),
            pltpu.VMEM((micros, max(chips - 1, 1), everyone, rows), jnp.bfloat16),
            pltpu.VMEM((micros, everyone, rows), jnp.float32),
            dma((2, micros, parts - 1)),
            dma((2, micros, parts - 1)),
            dma((2, micros)),
            dma((2, micros, max(chips - 1, 1))),
            dma((2, micros, chips)),
            dma((2, micros, max(chips - 1, 1))),
            dma((2, micros)),
            dma((2, micros, parts - 1)),
        ]
    vmem = pl.BlockSpec(memory_space=pltpu.VMEM)
    return pl.pallas_call(
        functools.partial(kernel, sections, parts, micros),
        out_shape=outs,
        in_specs=[vmem] * len(operands),
        out_specs=[vmem] * len(outs),
        scratch_shapes=scratch,
        compiler_params=pltpu.CompilerParams(
            collective_id=0, has_side_effects=True, vmem_limit_bytes=60 * 1024 * 1024
        ),
    )(*operands)


def finish_kernel(scale, *refs):
    outs, buffers, sems = refs[6:10], refs[10:14], refs[14]
    staged, in_sems = refs[15:21], refs[21]
    loads = [pltpu.make_async_copy(refs[i], staged[i], in_sems.at[i]) for i in range(6)]
    for i in (3, 4, 5, 0, 1, 2):
        loads[i].start()
    pending = []

    def flush(src, dst):
        copy = pltpu.make_async_copy(src, dst, sems.at[len(pending)])
        copy.start()
        pending.append(copy)

    for b in (1, 0):
        grads_in, columns, local = staged[3 * b : 3 * b + 3]
        for load in loads[3 * b : 3 * b + 3]:
            load.wait()
        grads, sums = outs[2 * b : 2 * b + 2]
        grad_buffer, sum_buffer = buffers[2 * b : 2 * b + 2]
        micros, parts, tokens, rows = columns.shape
        for part in range(parts):
            grad_buffer[:, :, part * rows : (part + 1) * rows] = grads_in[part]
        flush(grad_buffer, grads)
        lefts = [columns[:, group].reshape(micros * tokens, rows) for group in range(parts)]
        for part in range(parts):
            span = pl.ds(part * rows, rows)
            total = None
            for group in range(parts):
                right = local[:, part, group * tokens : (group + 1) * tokens]
                term = lax.dot_general(
                    lefts[group], right.reshape(micros * tokens, rows), (((0,), (0,)), ((), ())),
                    preferred_element_type=jnp.float32,
                )
                term = (term * scale).astype(jnp.bfloat16).astype(jnp.float32)
                total = term if total is None else total + term
            sum_buffer[:, part * rows : (part + 1) * rows] = total
            if rows % 128 == 0:
                flush(sum_buffer.at[:, span], sums.at[:, span])
        if rows % 128:
            flush(sum_buffer, sums)
    for copy in pending:
        copy.wait()


def finish(results, scale):
    outs, buffers = [], []
    for b in range(2):
        parts, micros, tokens, rows = results[3 * b].shape
        shapes = [((micros, tokens, parts * rows), jnp.bfloat16), ((rows, parts * rows), jnp.float32)]
        outs += [jax.ShapeDtypeStruct(*shape) for shape in shapes]
        buffers += [pltpu.VMEM(*shape) for shape in shapes]
    return pl.pallas_call(
        functools.partial(finish_kernel, scale),
        out_shape=outs,
        in_specs=[pl.BlockSpec(memory_space=pl.ANY)] * 6,
        out_specs=[pl.BlockSpec(memory_space=pl.ANY)] * 4,
        scratch_shapes=buffers
        + [pltpu.SemaphoreType.DMA((2 * parts + 4,))]
        + [pltpu.VMEM(result.shape, result.dtype) for result in results]
        + [pltpu.SemaphoreType.DMA((6,))],
        compiler_params=pltpu.CompilerParams(vmem_limit_bytes=63 * 1024 * 1024),
    )(*results)


def shards(vit_weight, t5_weight, vit_saved, t5_saved, vit_top_grad, t5_top_grad):
    sections = lax.axis_size("section")
    micros, tokens = t5_top_grad.shape[:2]
    scale = 1.0 / (micros * tokens)
    cut = 2 if tokens % 32 == 0 else 1

    def chunks(block):
        return block.reshape(micros * cut, tokens // cut, -1)

    results = branch_call(
        sections,
        [t5_weight[0], vit_weight[0]],
        [chunks(t5_saved[0]), chunks(vit_saved[0])],
        [chunks(t5_top_grad), chunks(vit_top_grad)],
    )
    t5_grads, t5_sum, vit_grads, vit_sum = finish(results, scale)
    return (
        vit_grads.reshape(vit_saved.shape),
        t5_grads.reshape(t5_saved.shape),
        vit_sum[None],
        t5_sum[None],
    )


def solution(mesh):
    placed = (
        P("section", "dp", None),
        P("section", "dp", None),
        P("section", None, "dp", None),
        P("section", None, "dp", None),
        P(None, "dp", None),
        P(None, "dp", None),
    )
    return jax.shard_map(
        shards,
        mesh=mesh,
        in_specs=placed,
        out_specs=(
            P("section", None, "dp", None),
            P("section", None, "dp", None),
            P("section", "dp", None),
            P("section", "dp", None),
        ),
        check_vma=False,
    )
```

profile of v0, /device:TPU:0, one launch (start us, length us, event | category | flops | bytes accessed | tf_op | source)
XLA Modules:
  0.0 152.5 jit_solution(179662997919391391)
XLA Ops:
  0.6 145.3 %shard_map.93 = (bf16[4,8,16,512]{3,2,1,0:T(8,128)(2,1)}, bf16[8,4,16,512]{3,2,1,0:T(8,128)(2,1)}, bf16[8,4,64,512]{3,2,1,0:T(8,128)(2,1)}, bf16[4,8,16,320]{3,2...) custom-call(bf16[512,2048]{1,0:T(8,128)(2,1)} %bitcast.10, ...), custom_call_target="tpu_custom_call" | custom-call | tf_op jit(solution)/shard_map/pallas_call | solution.py:394
  145.9 6.6 %shard_map.94 = (bf16[8,16,2048]{2,1,0:T(8,128)(2,1)}, f32[512,2048]{1,0:T(8,128)}, bf16[8,16,1280]{2,1,0:T(8,128)(2,1)}, f32[320,1280]{1,0:T(8,128)}) custom-call(bf16[4,8,16,512]{3,2,1,0:T(8,128)(2,1)} %get-tuple-element.14.refs_0_, bf16[8,4,16,512]{3,2,1,0:T(8,128)(2,1)} %get-tuple-element.15.refs_1_, bf16[8,4,64,512]{3,2,1,0:T(8,128)(2,1)} %get-tuple-element.16.refs_2_, ...), custom_call_target="tpu_custom_call" | custom-call | tf_op jit(solution)/shard_map/pallas_call | solution.py:457
where the time goes:
time: 153 us
  Pallas kernels  152 us (99%)
    pallas_call x1, Pallas kernels, branch_call(): pl.pallas_call(functools.partial(kernel, sections, parts, micros), out_sh...  145 us
    pallas_call x1, Pallas kernels, finish(): pl.pallas_call(functools.partial(finish_kernel, scale), out_shape=outs, i...  6.64 us

commit v1 on v0

v1 whole, which is shorter than its diff:
```python
import functools

import jax
import jax.numpy as jnp
from jax import lax
from jax.experimental import pallas as pl
from jax.experimental.pallas import tpu as pltpu
from jax.sharding import PartitionSpec as P

root_half = 0.7071067811865476
inv_root_tau = 0.3989422804014327
MESH = pl.DeviceIdType.MESH


def gelu_slope(preact):
    cumulative = 0.5 * (1.0 + lax.erf(preact * root_half))
    density = jnp.exp(-0.5 * preact * preact) * inv_root_tau
    return cumulative + preact * density


NAMES = (
    "saved", "top", "lifted", "columns", "local", "weight", "flip", "above", "below", "mine",
    "pair_out", "pair_in", "chip_in", "slopes", "sums", "saved_got", "above_got", "pair_got",
    "chip_got", "near_got", "far_got", "slope_got", "out_got", "sent", "top_sent", "top_got",
    "lift_sent",
)
SENDS = ("saved", "pair", "chip", "near", "far", "slope", "hop", "out", "columns", "local", "sums")


class Branch:
    def __init__(self, ins, outs, scratch):
        self.weight_in, self.saved_in, self.top_in = ins
        self.out, self.columns_out, self.local_out, self.sums_out = outs
        for name, ref in zip(NAMES, scratch):
            setattr(self, name, ref)


def drain(ref, sem):
    pltpu.make_async_copy(ref, ref, sem).wait()


def kernel(sections, parts, size, roomy, scale, *refs):
    ins, outs, scratch = refs[:6], refs[6:14], refs[14:]
    branches = [
        Branch(ins[3 * b : 3 * b + 3], outs[4 * b : 4 * b + 4],
               scratch[len(NAMES) * b : len(NAMES) * (b + 1)])
        for b in range(2)
    ]
    count = size * parts
    first_size = size // 2 if size % 2 == 0 else size
    section = lax.axis_index("section")
    me = lax.axis_index("dp")
    chips = parts // 2
    chip, core = me // 2, me % 2
    partner = chip * 2 + 1 - core
    last = sections - 1
    is_last = section == last
    is_first = section == 0
    wide_count = sections // 2 + 1 if roomy else 0
    wide_flag = lax.min(lax.max(wide_count - section, 0), 1)
    wide_in = section < wide_count
    wide_out = jnp.logical_and(section > 0, section <= wide_count)
    lag = lax.min(1 + (2 - 1) * lax.max(section - last + 1, 0), count)
    narrow_sums = lax.min(3 + 4 * (last - section) * (last - section), count)
    first_sums = narrow_sums + (min(4, count) - narrow_sums) * wide_flag

    def slot(part):
        return part if roomy else 0

    def ahead(k):
        return lax.rem(chip + k, chips) * 2 + core

    def behind(k):
        return lax.rem(chip + chips - k, chips) * 2 + core

    def other(group):
        return group + 1 - 2 * core

    def owner(m):
        turn = m // size
        return lax.rem(turn, chips) * 2 + 1 - turn // chips

    def copy(src, dst, sent, got, where, part):
        return pltpu.make_async_remote_copy(
            src_ref=src, dst_ref=dst, send_sem=sent, recv_sem=got,
            device_id=(where, part), device_id_type=MESH,
        )

    def sent(br, name):
        return br.sent.at[SENDS.index(name)]

    def padded(block, wide):
        spare = wide - block.shape[-1]
        if spare:
            block = jnp.concatenate([block, jnp.zeros((*block.shape[:-1], spare), block.dtype)], axis=-1)
        return block

    def regroup(source, groups):
        cut = source.shape[-1] // parts
        for group in range(parts):
            groups[group] = padded(source[..., group * cut : (group + 1) * cut], groups.shape[-1])

    barrier = pltpu.get_barrier_semaphore()
    for k in range(1, parts):
        pl.semaphore_signal(barrier, inc=1, device_id=(section, lax.rem(me + k, parts)), device_id_type=MESH)

    def greet(other_section):
        for part in range(parts):
            pl.semaphore_signal(barrier, inc=1, device_id=(other_section, part), device_id_type=MESH)

    @pl.when(is_last)
    def _():
        @pl.loop(0, last)
        def _(lower):
            pl.semaphore_signal(barrier, inc=1, device_id=(lower, me), device_id_type=MESH)

    @pl.when(jnp.logical_not(is_last))
    def _():
        greet(section + 1)

    with jax.named_scope("regroup_saved"):
        for br in branches:
            regroup(br.saved_in, br.saved)
            regroup(br.top_in, br.top)
    greeted = parts * lax.min(section, 1) + lax.min(last - section, 1)
    with jax.named_scope("barrier"):
        pl.semaphore_wait(barrier, parts - 1 + greeted)

    def helper(m):
        return last - lax.rem(m, sections)

    def saved_copy(br, turn, k):
        to = lax.rem(me + k, parts)
        return copy(br.saved.at[to], br.columns.at[turn], sent(br, "saved"), br.saved_got.at[turn], section, to)

    def top_copy(br, m, k):
        to, turn = lax.rem(me + k, parts), m // sections
        return copy(br.top.at[to, lax.rem(m, size)], br.lifted.at[turn], br.top_sent.at[turn], br.top_got.at[turn], section, to)

    def lift_copy(br, m):
        turn = m // sections
        return copy(br.lifted.at[turn], br.above.at[m, slot(me)], br.lift_sent.at[turn], br.above_got.at[m], last, me)

    def pair_copy(br, m):
        return copy(br.pair_out.at[m], br.pair_in.at[m], sent(br, "pair"), br.pair_got.at[m], section, partner)

    def chip_copy(br, m, k):
        return copy(br.mine.at[m, k], br.chip_in.at[m, k - 1], sent(br, "chip"), br.chip_got.at[m], section, ahead(k))

    def near_copy(br, m, k):
        group = behind(k)
        return copy(br.local.at[m, group], br.local.at[m, group], sent(br, "near"), br.near_got.at[m], section, partner)

    def far_copy(br, m, k):
        return copy(br.local.at[m, me], br.local.at[m, me], sent(br, "far"), br.far_got.at[m], section, ahead(k))

    def hop_copy(br, m, k):
        return copy(br.below.at[m], br.above.at[m, slot(me)], sent(br, "hop"), br.above_got.at[m], lax.max(section - 1, 0), ahead(k))

    def share_copy(br, m, k):
        group = behind(k)
        return copy(br.above.at[m, group], br.above.at[m, group], sent(br, "near"), br.near_got.at[m], section, partner)

    def slope_far(br, m, k):
        return copy(br.slopes.at[m, me], br.slopes.at[m, me], sent(br, "far"), br.far_got.at[m], section, ahead(k))

    def slope_near(br, m, k):
        group = behind(k)
        return copy(br.slopes.at[m, group], br.slopes.at[m, group], sent(br, "slope"), br.slope_got.at[m], section, partner)

    def out_copy(br, m):
        return copy(br.below.at[m], br.out.at[me, lax.rem(m, size)], sent(br, "out"), br.out_got.at[0], section, owner(m))

    def half_copy(br, h, k):
        to, span = lax.rem(me + k, parts), pl.ds(h * first_size, first_size)
        return copy(br.saved.at[to, span], br.columns.at[0, span], sent(br, "saved"), br.saved_got.at[h * parts], section, to)

    def piecewise(turn):
        return jnp.logical_and(is_last, turn == chips)

    def piece_copy(br, m, k):
        to, turn, at = lax.rem(me + k, parts), m // size, lax.rem(m, size)
        return copy(br.saved.at[to, at], br.columns.at[turn, at], sent(br, "saved"), br.saved_got.at[turn], section, to)

    def send_piece(m):
        @pl.when(jnp.logical_and(piecewise(m // size), owner(m) == me))
        def _():
            for br in branches:
                for k in range(1, parts):
                    piece_copy(br, m, k).start()

    def send_saved(first, end):
        @pl.loop(first, end)
        def _(turn):
            @pl.when(owner(turn * size) == me)
            def _():
                for br in branches:
                    br.columns[turn] = br.saved[me]

                @pl.when(turn == 0)
                def _():
                    @pl.loop(0, size // first_size)
                    def _(h):
                        for br in branches:
                            for k in range(1, parts):
                                half_copy(br, h, k).start()

                @pl.when(jnp.logical_and(turn > 0, jnp.logical_not(piecewise(turn))))
                def _():
                    for br in branches:
                        for k in range(1, parts):
                            saved_copy(br, turn, k).start()

    def send_tops(first, end):
        @pl.loop(first, end)
        def _(m):
            @pl.when(jnp.logical_and(helper(m) == section, owner(m) == me))
            def _():
                for br in branches:
                    br.lifted[m // sections] = br.top[me, lax.rem(m, size)]
                    for k in range(1, parts):
                        top_copy(br, m, k).start()

    def wait_top(br, m):
        @pl.when(owner(m) != me)
        def _():
            drain(br.lifted.at[m // sections], br.top_got.at[m // sections])

    def lift(first, end):
        @pl.loop(first, end)
        def _(m):
            @pl.when(helper(m) == section)
            def _():
                for br in branches:
                    wait_top(br, m)
                    lift_copy(br, m).start()

    def partial_of(turn, at, length, got):
        first = turn * size + at

        @pl.when(owner(turn * size) != me)
        def _():
            for br in branches:
                drain(br.columns.at[turn, pl.ds(at, length)], br.saved_got.at[got])

        span = pl.ds(first, length)
        for br in branches:
            wide = br.columns.shape[-1]
            tokens = br.columns[turn, pl.ds(at, length)].reshape(-1, wide)

            def product(group):
                block = jnp.dot(tokens, br.weight[group], preferred_element_type=jnp.float32)
                return block.astype(jnp.bfloat16).reshape(length, -1, wide)

            for k in range(chips):
                br.pair_out[span, k] = product(other(ahead(k)))

            @pl.loop(first, first + length)
            def _(m):
                pair_copy(br, m).start()

            for k in range(chips):
                br.mine[span, k] = product(ahead(k))

    @jax.named_scope("partial")
    def partial(turn):
        partial_of(turn, 0, size, turn)

    def pair_sum(m):
        for br in branches:
            drain(br.pair_in.at[m], br.pair_got.at[m])
            for k in range(1, chips):
                both = br.mine[m, k].astype(jnp.float32) + br.pair_in[m, k].astype(jnp.float32)
                br.mine[m, k] = both.astype(jnp.bfloat16)
                chip_copy(br, m, k).start()

    def find_slope(br, m):
        total = br.mine[m, 0].astype(jnp.float32) + br.pair_in[m, 0].astype(jnp.float32)
        if chips > 1:
            drain(br.chip_in.at[m], br.chip_got.at[m])
        for k in range(1, chips):
            total = total + br.chip_in[m, k - 1].astype(jnp.float32)
        br.slopes[m, slot(me)] = gelu_slope(total).astype(jnp.bfloat16)

    @jax.named_scope("spread")
    def spread(m):
        at_hand = jnp.logical_and(is_last, helper(m) == section)
        for br in branches:
            find_slope(br, m)

            @pl.when(at_hand)
            def _():
                wait_top(br, m)
                br.above[m, slot(me)] = br.lifted[m // sections]

            @pl.when(jnp.logical_not(at_hand))
            def _():
                drain(br.below.at[m], br.above_got.at[m])

            upper = br.above[m, slot(me)].astype(jnp.float32)
            br.local[m, me] = (upper * br.slopes[m, slot(me)].astype(jnp.float32)).astype(jnp.bfloat16)
            for k in range(1, chips):
                far_copy(br, m, k).start()
            near_copy(br, m, 0).start()

    @jax.named_scope("relay")
    def relay(m):
        for br in branches:
            if chips > 1:
                drain(br.local.at[m, pl.ds(0, chips - 1)], br.far_got.at[m])
            for k in range(1, chips):
                near_copy(br, m, k).start()

    def through(br, m, blocks):
        total = jnp.dot(jnp.concatenate(blocks, axis=-1), br.flip[...], preferred_element_type=jnp.float32)
        total = br.above[m, slot(me)].astype(jnp.float32) + total
        br.below[m] = total.astype(jnp.bfloat16)

        @pl.when(jnp.logical_not(is_first))
        def _():
            hop_copy(br, m, 0).start()

        @pl.when(wide_out)
        def _():
            for k in range(1, chips):
                hop_copy(br, m, k).start()

    @jax.named_scope("descend")
    def descend(m):
        for br in branches:
            drain(br.local.at[m, pl.ds(0, chips)], br.near_got.at[m])
            through(br, m, [br.local[m, group] for group in range(parts)])

    @jax.named_scope("share")
    def share(m):
        for br in branches:
            drain(br.local.at[m, pl.ds(0, chips)], br.above_got.at[m])
            for k in range(chips):
                share_copy(br, m, k).start()

    @jax.named_scope("descend_wide")
    def descend_wide(m):
        for br in branches:
            drain(br.local.at[m, pl.ds(0, chips)], br.slope_got.at[m])
            drain(br.local.at[m, pl.ds(0, chips)], br.near_got.at[m])
            blocks = []
            for group in range(parts):
                block = br.above[m, group].astype(jnp.float32) * br.slopes[m, group].astype(jnp.float32)
                blocks.append(block.astype(jnp.bfloat16))
                br.local[m, group] = blocks[-1]
            through(br, m, blocks)

    def hand_out(m):
        for br in branches:
            @pl.when(owner(m) == me)
            def _():
                br.out[me, lax.rem(m, size)] = br.below[m]

            @pl.when(owner(m) != me)
            def _():
                out_copy(br, m).start()

    @jax.named_scope("sums")
    def add_sums(m):
        if not roomy:
            return
        turn, group = m // size - 1, lax.rem(m, size)

        @pl.when(turn >= 0)
        def _():
            span = pl.ds(lax.max(turn, 0) * size, size)
            for br in branches:
                wide = br.columns.shape[-1]
                left = br.columns[lax.max(turn, 0)].reshape(-1, wide)
                right = br.local[span, group].reshape(-1, wide)
                term = lax.dot_general(left, right, (((0,), (0,)), ((), ())), preferred_element_type=jnp.float32)
                br.sums[group] = br.sums[group] + (term * scale).astype(jnp.bfloat16).astype(jnp.float32)

                @pl.when(turn == parts - 2)
                def _():
                    pltpu.make_async_copy(br.sums.at[group], br.sums_out.at[group], sent(br, "sums")).start()

    early = min(sections, count)

    @pl.when(jnp.logical_not(is_last))
    def _():
        send_tops(0, early)

    send_saved(0, parts)

    @pl.when(is_last)
    def _():
        send_tops(0, early)

    send_tops(early, count)

    with jax.named_scope("regroup_weight"):
        for br in branches:
            rows = br.weight_in.shape[0]
            wide = br.weight.shape[-1]
            for group in range(parts):
                block = padded(br.weight_in[:, group * rows : (group + 1) * rows], wide)
                br.weight[group, :rows] = block
                if wide > rows:
                    br.weight[group, rows:] = jnp.zeros((wide - rows, wide), block.dtype)

    with jax.named_scope("flip_weight"):
        for br in branches:
            wide = br.weight.shape[-1]

            @pl.loop(0, parts)
            def _(group):
                br.flip[pl.ds(pl.multiple_of(group * wide, 128), wide), :] = br.weight[group].T
                if roomy:
                    br.sums[group] = jnp.zeros((wide, wide), jnp.float32)

    @pl.when(jnp.logical_not(is_last))
    def _():
        lift(0, early)

    @pl.loop(0, size // first_size)
    def _(h):
        with jax.named_scope("first_partial"):
            partial_of(0, h * first_size, first_size, h * parts)
        pl.loop(h * first_size, lax.min(first_sums, (h + 1) * first_size))(pair_sum)

    @pl.loop(0, max(size - 1, 1))
    def _(at):
        send_piece(at + chips * size)

    @pl.when(jnp.logical_not(is_last))
    def _():
        lift(early, count)
        pl.loop(1, parts)(partial)
        pl.loop(size, lax.max(first_sums, size))(pair_sum)

    def mixed(i):
        pair, at = i // (2 * size), lax.rem(i, 2 * size)
        return pair * 2 * size + lax.rem(at, 2) * size + at // 2

    def run_narrow():
        @pl.loop(0, count + lag + 1)
        def _(step):
            @pl.when(step < count)
            def _():
                spread(step)

            @pl.when(step < count - first_sums)
            def _():
                pair_sum(step + first_sums)

            @pl.when(step < size - max(size - 1, 1))
            def _():
                send_piece(chips * size + max(size - 1, 1) + step)

            @pl.when(jnp.logical_and(is_last, jnp.logical_and(step < count - size, lax.rem(step, size) == 0)))
            def _():
                partial(step // size + 1)

            @pl.when(jnp.logical_and(step > lag, step < count + lag + 1))
            def _():
                descend(step - lag - 1)

            @pl.when(jnp.logical_and(step >= lag, step < count + lag))
            def _():
                relay(step - lag)

            @pl.when(step > lag)
            def _():
                add_sums(step - lag - 1)

        pl.loop(0, count)(lambda i: hand_out(mixed(i)))

    def run_wide():
        def prepare(m):
            @pl.when(m < count)
            def _():
                for br in branches:
                    find_slope(br, m)
                    for k in range(1, chips):
                        slope_far(br, m, k).start()
                    slope_near(br, m, 0).start()

            @pl.when(m < count - first_sums)
            def _():
                pair_sum(m + first_sums)

            @pl.when(m >= 2)
            def _():
                for br in branches:
                    if chips > 1:
                        drain(br.local.at[m - 2, pl.ds(0, chips - 1)], br.far_got.at[m - 2])
                    for k in range(1, chips):
                        slope_near(br, m - 2, k).start()

        start = lax.min(10 + 2 * (wide_count - 1 - section), count + 2)
        with jax.named_scope("prepare"):
            pl.loop(0, start)(prepare)

        @pl.loop(0, count)
        def _(m):
            share(m)

            @pl.when(m > 0)
            def _():
                add_sums(lax.max(m - 1, 0))

            descend_wide(m)

            @pl.when(is_first)
            def _():
                hand_out(m)

            @pl.when(jnp.logical_and(section == 1, m >= size))
            def _():
                hand_out(mixed(lax.max(m - size, 0)))

            @pl.when(m + start < count + 2)
            def _():
                prepare(m + start)

        @pl.when(section == 1)
        def _():
            pl.loop(count - size, count)(lambda i: hand_out(mixed(i)))

        @pl.when(section > 1)
        def _():
            pl.loop(0, count)(lambda i: hand_out(mixed(i)))

        add_sums(count - 1)

    if roomy:
        pl.when(jnp.logical_not(wide_in))(run_narrow)
        pl.when(wide_in)(run_wide)
    else:
        run_narrow()

    with jax.named_scope("final_waits"):
        for br in branches:
            kept = br.columns_out.shape[0]
            columns = br.columns.at[pl.ds(parts - kept, kept)]
            pltpu.make_async_copy(columns, br.columns_out, sent(br, "columns")).start()
            local = br.local.at[pl.ds(count - kept * size, kept * size)]
            pltpu.make_async_copy(local, br.local_out, sent(br, "local")).start()
        for br in branches:
            others = pl.ds(0, parts - 1)
            drain(br.saved.at[others], sent(br, "saved"))
            drain(br.pair_in, sent(br, "pair"))
            drain(br.local.at[:, pl.ds(0, chips)], sent(br, "near"))
            if chips > 1:
                drain(br.chip_in, sent(br, "chip"))
                drain(br.local.at[:, pl.ds(0, chips - 1)], sent(br, "far"))

            if roomy:
                @pl.when(wide_in)
                def _():
                    drain(br.local.at[:, pl.ds(0, chips)], sent(br, "slope"))

                @pl.when(wide_out)
                def _():
                    drain(br.local.at[:, pl.ds(0, chips)], sent(br, "hop"))

                drain(br.sums, sent(br, "sums"))

            @pl.when(section > wide_count)
            def _():
                drain(br.below, sent(br, "hop"))

        @pl.loop(0, count)
        def _(m):
            @pl.when(jnp.logical_and(helper(m) == section, owner(m) == me))
            def _():
                for br in branches:
                    drain(br.top.at[pl.ds(0, parts - 1), 0], br.top_sent.at[m // sections])

            @pl.when(jnp.logical_and(jnp.logical_not(is_last), helper(m) == section))
            def _():
                for br in branches:
                    drain(br.lifted.at[m // sections], br.lift_sent.at[m // sections])

        for br in branches:
            drain(br.columns_out, sent(br, "columns"))
            drain(br.local_out, sent(br, "local"))
            drain(br.below.at[pl.ds(0, count - size)], sent(br, "out"))
            drain(br.out.at[pl.ds(0, parts - 1)], br.out_got.at[0])


def branch_call(sections, scale, weights, saveds, tops):
    half, full = jnp.bfloat16, jnp.float32
    operands, outs, out_specs, scratch = [], [], [], []
    vmem = pl.BlockSpec(memory_space=pltpu.VMEM)
    anywhere = pl.BlockSpec(memory_space=pl.ANY)
    rows, width = weights[0].shape
    parts = width // rows
    size, tokens = saveds[0].shape[:2]
    volume = sum(saved.size * saved.dtype.itemsize for saved in saveds)
    roomy = parts == size and volume * parts <= 8 * 1024 * 1024
    chips = parts // 2
    count = size * parts
    kept = 1 if roomy else parts
    turns = -(-count // sections)
    for weight, saved, top in zip(weights, saveds, tops):
        wide = -(-weight.shape[0] // 128) * 128
        operands += [weight, saved, top]
        all_sums = (parts, wide, wide) if roomy else (1, 8, 128)
        outs += [
            jax.ShapeDtypeStruct((parts, size, tokens, wide), half),
            jax.ShapeDtypeStruct((kept, size, tokens, wide), half),
            jax.ShapeDtypeStruct((kept * size, parts, tokens, wide), half),
            jax.ShapeDtypeStruct(all_sums, full),
        ]
        out_specs += [vmem, anywhere, anywhere, anywhere]
        dma = pltpu.SemaphoreType.DMA
        slots = parts if roomy else 1
        scratch += [
            pltpu.VMEM((parts, size, tokens, wide), half),
            pltpu.VMEM((parts, size, tokens, wide), half),
            pltpu.VMEM((turns, tokens, wide), half),
            pltpu.VMEM((parts, size, tokens, wide), half),
            pltpu.VMEM((count, parts, tokens, wide), half),
            pltpu.VMEM((parts, wide, wide), half),
            pltpu.VMEM((parts * wide, wide), half),
            pltpu.VMEM((count, slots, tokens, wide), half),
            pltpu.VMEM((count, tokens, wide), half),
            pltpu.VMEM((count, chips, tokens, wide), half),
            pltpu.VMEM((count, chips, tokens, wide), half),
            pltpu.VMEM((count, chips, tokens, wide), half),
            pltpu.VMEM((count, max(chips - 1, 1), tokens, wide), half),
            pltpu.VMEM((count, slots, tokens, wide), half),
            pltpu.VMEM(all_sums, full),
            dma((parts + 1,)),
            dma((count,)),
            dma((count,)),
            dma((count,)),
            dma((count,)),
            dma((count,)),
            dma((count if roomy else 1,)),
            dma((1,)),
            dma((len(SENDS),)),
            dma((turns,)),
            dma((turns,)),
            dma((turns,)),
        ]
    return roomy, pl.pallas_call(
        functools.partial(kernel, sections, parts, size, roomy, scale),
        out_shape=outs,
        in_specs=[vmem] * len(operands),
        out_specs=out_specs,
        scratch_shapes=scratch,
        compiler_params=pltpu.CompilerParams(
            collective_id=0, has_side_effects=True, vmem_limit_bytes=63 * 1024 * 1024
        ),
    )(*operands)


def finish_kernel(roomy, scale, *refs):
    outs, buffers, sems = refs[8:12], refs[12:16], refs[16]
    staged, in_sems = refs[17:25], refs[25]
    pending = []

    def load(i, *at):
        src, dst = (refs[i].at[at], staged[i].at[at]) if at else (refs[i], staged[i])
        return pltpu.make_async_copy(src, dst, in_sems.at[(i, *(at or (0,)))])

    def flush(src, dst):
        copy = pltpu.make_async_copy(src, dst, sems.at[len(pending)])
        copy.start()
        pending.append(copy)

    parts = staged[0].shape[0]
    for b in (1, 0):
        load(4 * b + 1).start()
        load(4 * b + 2).start()
        if roomy:
            for part in range(parts):
                load(4 * b + 3, part).start()
        load(4 * b).start()

    for b in (1, 0):
        grads_in, columns, local, sums_in = staged[4 * b : 4 * b + 4]
        grads, sums = outs[2 * b : 2 * b + 2]
        grad_buffer, sum_buffer = buffers[2 * b : 2 * b + 2]
        _, size, tokens, wide = grads_in.shape
        rows = sum_buffer.shape[0]
        load(4 * b + 1).wait()
        load(4 * b + 2).wait()
        spans = [slice(turn * size, (turn + 1) * size) for turn in range(columns.shape[0])]
        lefts = [columns[turn].reshape(size * tokens, wide)[:, :rows] for turn in range(columns.shape[0])]
        for part in range(parts):
            total = None
            for left, span in zip(lefts, spans):
                right = local[span, part].reshape(size * tokens, wide)[:, :rows]
                term = lax.dot_general(
                    left, right, (((0,), (0,)), ((), ())), preferred_element_type=jnp.float32,
                )
                term = (term * scale).astype(jnp.bfloat16).astype(jnp.float32)
                total = term if total is None else total + term
            if roomy:
                load(4 * b + 3, part).wait()
                total = sums_in[part, :rows, :rows] + total
            sum_buffer[:, part * rows : (part + 1) * rows] = total
            if rows % 128 == 0:
                span = pl.ds(part * rows, rows)
                flush(sum_buffer.at[:, span], sums.at[:, span])
        if rows % 128:
            flush(sum_buffer, sums)
        load(4 * b).wait()
        for part in range(parts):
            grad_buffer[:, :, part * rows : (part + 1) * rows] = grads_in[part][..., :rows]
        flush(grad_buffer, grads)
    for copy in pending:
        copy.wait()


def finish(roomy, results, rows_of, scale):
    outs, buffers = [], []
    for b in range(2):
        parts, size, tokens, _ = results[4 * b].shape
        rows = rows_of[b]
        shapes = [((size, tokens, parts * rows), jnp.bfloat16), ((rows, parts * rows), jnp.float32)]
        outs += [jax.ShapeDtypeStruct(*shape) for shape in shapes]
        buffers += [pltpu.VMEM(*shape) for shape in shapes]
    return pl.pallas_call(
        functools.partial(finish_kernel, roomy, scale),
        out_shape=outs,
        in_specs=[pl.BlockSpec(memory_space=pl.ANY)] * 8,
        out_specs=[pl.BlockSpec(memory_space=pl.ANY)] * 4,
        scratch_shapes=buffers
        + [pltpu.SemaphoreType.DMA((2 * parts + 4,))]
        + [pltpu.VMEM(result.shape, result.dtype) for result in results]
        + [pltpu.SemaphoreType.DMA((8, parts))],
        compiler_params=pltpu.CompilerParams(vmem_limit_bytes=63 * 1024 * 1024),
    )(*results)


def shards(vit_weight, t5_weight, vit_saved, t5_saved, vit_top_grad, t5_top_grad):
    sections = lax.axis_size("section")
    size, tokens = t5_top_grad.shape[:2]
    scale = 1.0 / (size * tokens)
    roomy, results = branch_call(
        sections,
        scale,
        [t5_weight[0], vit_weight[0]],
        [t5_saved[0], vit_saved[0]],
        [t5_top_grad, vit_top_grad],
    )
    t5_grads, t5_sum, vit_grads, vit_sum = finish(
        roomy, results, [t5_weight.shape[1], vit_weight.shape[1]], scale
    )
    return vit_grads[None], t5_grads[None], vit_sum[None], t5_sum[None]


def solution(mesh):
    placed = (
        P("section", "dp", None),
        P("section", "dp", None),
        P("section", None, "dp", None),
        P("section", None, "dp", None),
        P(None, "dp", None),
        P(None, "dp", None),
    )
    return jax.shard_map(
        shards,
        mesh=mesh,
        in_specs=placed,
        out_specs=(
            P("section", None, "dp", None),
            P("section", None, "dp", None),
            P("section", "dp", None),
            P("section", "dp", None),
        ),
        check_vma=False,
    )
```

time: 153 us -> 129 us (0.84)
  Pallas kernels: 152 us -> 128 us
    pallas_call x2, Pallas kernels: 152 us -> 128 us  [the longest x1 123 us: branch_call(): pl.pallas_call(functools.partial(kernel, sections, parts, size, roomy, sc...]
where the time goes in v1:
time: 129 us
  Pallas kernels  128 us (99%)
    pallas_call x1, Pallas kernels, branch_call(): pl.pallas_call(functools.partial(kernel, sections, parts, size, roomy, sc...  123 us
    pallas_call x1, Pallas kernels, finish(): pl.pallas_call(functools.partial(finish_kernel, roomy, scale), out_shape=...  5.59 us

profile of v1, /device:TPU:0, one launch (start us, length us, event | category | flops | bytes accessed | tf_op | source)
XLA Modules:
  0.0 129.0 jit_solution(3098344189530435350)
XLA Ops:
  0.6 122.7 %shard_map.93 = (bf16[4,4,32,512]{3,2,1,0:T(8,128)(2,1)}, bf16[1,4,32,512]{3,2,1,0:T(8,128)(2,1)}, bf16[4,4,32,512]{3,2,1,0:T(8,128)(2,1)}, f32[4,512,512]{2,1,0...) custom-call(bf16[512,2048]{1,0:T(8,128)(2,1)} %bitcast.8, ...), custom_call_target="tpu_custom_call" | custom-call | tf_op jit(solution)/shard_map/pallas_call | solution.py:644
  123.4 5.6 %shard_map.94 = (bf16[4,32,2048]{2,1,0:T(8,128)(2,1)}, f32[512,2048]{1,0:T(8,128)}, bf16[4,32,1280]{2,1,0:T(8,128)(2,1)}, f32[320,1280]{1,0:T(8,128)}) custom-call(bf16[4,4,32,512]{3,2,1,0:T(8,128)(2,1)} %get-tuple-element.16.refs_0_, bf16[1,4,32,512]{3,2,1,0:T(8,128)(2,1)} %get-tuple-element.17.refs_1_, bf16[4,4,32,512]{3,2,1,0:T(8,128)(2,1)} %get-tuple-element.18.refs_2_, ...), custom_call_target="tpu_custom_call" | custom-call | tf_op jit(solution)/shard_map/pallas_call | solution.py:723

commit v2 on v1

--- a/solution.py
+++ b/solution.py
@@ -33,6 +33,36 @@
         self.out, self.columns_out, self.local_out, self.sums_out = outs
         for name, ref in zip(NAMES, scratch):
             setattr(self, name, ref)
+        self.rows = self.weight_in.shape[0]
+        self.tokens = self.saved_in.shape[1]
+        self.main, self.rest = layout(self.rows, self.tokens)
+
+
+def layout(rows, tokens):
+    main = rows // 128 * 128
+    rest = rows - main
+    if rest and main and main % rest == 0 and tokens % (8 * (main // rest)) == 0:
+        return main, rest
+    return -(-rows // 128) * 128, 0
+
+
+def fold(block, rest):
+    if rest == 0:
+        return block
+    main = block.shape[1] - rest
+    step = block.shape[0] * rest // main
+    pieces = [block[first : first + step, main:] for first in range(0, block.shape[0], step)]
+    return jnp.concatenate([block[:, :main], jnp.concatenate(pieces, axis=1)], axis=0)
+
+
+def unfold(block, rest):
+    if rest == 0:
+        return [block]
+    main = block.shape[1]
+    tokens = block.shape[0] * main // (main + rest)
+    tail = block[tokens:].astype(jnp.float32)
+    pieces = [tail[:, first : first + rest] for first in range(0, main, rest)]
+    return [block[:tokens], jnp.concatenate(pieces, axis=0).astype(block.dtype)]
 
 
 def drain(ref, sem):
@@ -60,7 +90,7 @@
     wide_flag = lax.min(lax.max(wide_count - section, 0), 1)
     wide_in = section < wide_count
     wide_out = jnp.logical_and(section > 0, section <= wide_count)
-    lag = lax.min(1 + (2 - 1) * lax.max(section - last + 1, 0), count)
+    lag = lax.min(1 + (1 - 1) * lax.max(section - last + 1, 0), count)
     narrow_sums = lax.min(3 + 4 * (last - section) * (last - section), count)
     first_sums = narrow_sums + (min(4, count) - narrow_sums) * wide_flag
 
@@ -95,6 +125,9 @@
             block = jnp.concatenate([block, jnp.zeros((*block.shape[:-1], spare), block.dtype)], axis=-1)
         return block
 
+    def packed(br, block):
+        return fold(block[:, : br.rows], br.rest) if br.rest else padded(block, br.main)
+
     def regroup(source, groups):
         cut = source.shape[-1] // parts
         for group in range(parts):
@@ -121,7 +154,10 @@
     with jax.named_scope("regroup_saved"):
         for br in branches:
             regroup(br.saved_in, br.saved)
-            regroup(br.top_in, br.top)
+            for group in range(parts):
+                for at in range(size):
+                    block = br.top_in[at, :, group * br.rows : (group + 1) * br.rows]
+                    br.top[group, at] = packed(br, block.astype(jnp.float32)).astype(jnp.bfloat16)
     greeted = parts * lax.min(section, 1) + lax.min(last - section, 1)
     with jax.named_scope("barrier"):
         pl.semaphore_wait(barrier, parts - 1 + greeted)
@@ -243,24 +279,25 @@
             for br in branches:
                 drain(br.columns.at[turn, pl.ds(at, length)], br.saved_got.at[got])
 
-        span = pl.ds(first, length)
         for br in branches:
             wide = br.columns.shape[-1]
             tokens = br.columns[turn, pl.ds(at, length)].reshape(-1, wide)
 
-            def product(group):
+            def product(into, k, group):
                 block = jnp.dot(tokens, br.weight[group], preferred_element_type=jnp.float32)
-                return block.astype(jnp.bfloat16).reshape(length, -1, wide)
+                for i in range(length):
+                    piece = packed(br, block[i * br.tokens : (i + 1) * br.tokens])
+                    into[first + i, k] = piece.astype(jnp.bfloat16)
 
             for k in range(chips):
-                br.pair_out[span, k] = product(other(ahead(k)))
+                product(br.pair_out, k, other(ahead(k)))
 
             @pl.loop(first, first + length)
             def _(m):
                 pair_copy(br, m).start()
 
             for k in range(chips):
-                br.mine[span, k] = product(ahead(k))
+                product(br.mine, k, ahead(k))
 
     @jax.named_scope("partial")
     def partial(turn):
@@ -312,8 +349,10 @@
                 near_copy(br, m, k).start()
 
     def through(br, m, blocks):
+        pieces = zip(*(unfold(block, br.rest) for block in blocks))
+        blocks = [block for piece in pieces for block in piece]
         total = jnp.dot(jnp.concatenate(blocks, axis=-1), br.flip[...], preferred_element_type=jnp.float32)
-        total = br.above[m, slot(me)].astype(jnp.float32) + total
+        total = br.above[m, slot(me)].astype(jnp.float32) + packed(br, total)
         br.below[m] = total.astype(jnp.bfloat16)
 
         @pl.when(jnp.logical_not(is_first))
@@ -368,11 +407,15 @@
 
         @pl.when(turn >= 0)
         def _():
-            span = pl.ds(lax.max(turn, 0) * size, size)
             for br in branches:
                 wide = br.columns.shape[-1]
                 left = br.columns[lax.max(turn, 0)].reshape(-1, wide)
-                right = br.local[span, group].reshape(-1, wide)
+                turn_start = lax.max(turn, 0) * size
+                right = jnp.concatenate(
+                    [jnp.concatenate(unfold(br.local[turn_start + i, group], br.rest), axis=-1) for i in range(size)],
+                    axis=0,
+                )
+                left, right = left[:, : br.rows], right[:, : br.rows]
                 term = lax.dot_general(left, right, (((0,), (0,)), ((), ())), preferred_element_type=jnp.float32)
                 br.sums[group] = br.sums[group] + (term * scale).astype(jnp.bfloat16).astype(jnp.float32)
 
@@ -410,9 +453,13 @@
 
             @pl.loop(0, parts)
             def _(group):
-                br.flip[pl.ds(pl.multiple_of(group * wide, 128), wide), :] = br.weight[group].T
+                turned = br.weight[group].T
+                br.flip[pl.ds(pl.multiple_of(group * br.main, 128), br.main), :] = turned[: br.main]
+                if br.rest:
+                    at = pl.multiple_of(parts * br.main + group * br.rest, br.rest)
+                    br.flip[pl.ds(at, br.rest), :] = turned[br.main : br.rows]
                 if roomy:
-                    br.sums[group] = jnp.zeros((wide, wide), jnp.float32)
+                    br.sums[group] = jnp.zeros(br.sums.shape[1:], jnp.float32)
 
     @pl.when(jnp.logical_not(is_last))
     def _():
@@ -600,13 +647,16 @@
     kept = 1 if roomy else parts
     turns = -(-count // sections)
     for weight, saved, top in zip(weights, saveds, tops):
-        wide = -(-weight.shape[0] // 128) * 128
+        rows = weight.shape[0]
+        wide = -(-rows // 128) * 128
+        main, rest = layout(rows, tokens)
+        block = (tokens + tokens * rest // main, main)
         operands += [weight, saved, top]
-        all_sums = (parts, wide, wide) if roomy else (1, 8, 128)
+        all_sums = (parts, rows, rows) if roomy else (1, 8, 128)
         outs += [
-            jax.ShapeDtypeStruct((parts, size, tokens, wide), half),
+            jax.ShapeDtypeStruct((parts, size, *block), half),
             jax.ShapeDtypeStruct((kept, size, tokens, wide), half),
-            jax.ShapeDtypeStruct((kept * size, parts, tokens, wide), half),
+            jax.ShapeDtypeStruct((kept * size, parts, *block), half),
             jax.ShapeDtypeStruct(all_sums, full),
         ]
         out_specs += [vmem, anywhere, anywhere, anywhere]
@@ -614,19 +664,19 @@
         slots = parts if roomy else 1
         scratch += [
             pltpu.VMEM((parts, size, tokens, wide), half),
+            pltpu.VMEM((parts, size, *block), half),
+            pltpu.VMEM((turns, *block), half),
             pltpu.VMEM((parts, size, tokens, wide), half),
-            pltpu.VMEM((turns, tokens, wide), half),
-            pltpu.VMEM((parts, size, tokens, wide), half),
-            pltpu.VMEM((count, parts, tokens, wide), half),
+            pltpu.VMEM((count, parts, *block), half),
             pltpu.VMEM((parts, wide, wide), half),
-            pltpu.VMEM((parts * wide, wide), half),
-            pltpu.VMEM((count, slots, tokens, wide), half),
-            pltpu.VMEM((count, tokens, wide), half),
-            pltpu.VMEM((count, chips, tokens, wide), half),
-            pltpu.VMEM((count, chips, tokens, wide), half),
-            pltpu.VMEM((count, chips, tokens, wide), half),
-            pltpu.VMEM((count, max(chips - 1, 1), tokens, wide), half),
-            pltpu.VMEM((count, slots, tokens, wide), half),
+            pltpu.VMEM((parts * (main + rest), wide), half),
+            pltpu.VMEM((count, slots, *block), half),
+            pltpu.VMEM((count, *block), half),
+            pltpu.VMEM((count, chips, *block), half),
+            pltpu.VMEM((count, chips, *block), half),
+            pltpu.VMEM((count, chips, *block), half),
+            pltpu.VMEM((count, max(chips - 1, 1), *block), half),
+            pltpu.VMEM((count, slots, *block), half),
             pltpu.VMEM(all_sums, full),
             dma((parts + 1,)),
             dma((count,)),
@@ -680,16 +730,22 @@
         grads_in, columns, local, sums_in = staged[4 * b : 4 * b + 4]
         grads, sums = outs[2 * b : 2 * b + 2]
         grad_buffer, sum_buffer = buffers[2 * b : 2 * b + 2]
-        _, size, tokens, wide = grads_in.shape
+        size, tokens = grad_buffer.shape[:2]
+        wide = columns.shape[-1]
         rows = sum_buffer.shape[0]
+        rest = layout(rows, tokens)[1]
+
+        def whole(block):
+            return jnp.concatenate(unfold(block, rest), axis=-1)[:, :rows]
+
         load(4 * b + 1).wait()
         load(4 * b + 2).wait()
-        spans = [slice(turn * size, (turn + 1) * size) for turn in range(columns.shape[0])]
+        spans = [range(turn * size, (turn + 1) * size) for turn in range(columns.shape[0])]
         lefts = [columns[turn].reshape(size * tokens, wide)[:, :rows] for turn in range(columns.shape[0])]
         for part in range(parts):
             total = None
             for left, span in zip(lefts, spans):
-                right = local[span, part].reshape(size * tokens, wide)[:, :rows]
+                right = jnp.concatenate([whole(local[i, part]) for i in span], axis=0)
                 term = lax.dot_general(
                     left, right, (((0,), (0,)), ((), ())), preferred_element_type=jnp.float32,
                 )
@@ -697,7 +753,7 @@
                 total = term if total is None else total + term
             if roomy:
                 load(4 * b + 3, part).wait()
-                total = sums_in[part, :rows, :rows] + total
+                total = sums_in[part] + total
             sum_buffer[:, part * rows : (part + 1) * rows] = total
             if rows % 128 == 0:
                 span = pl.ds(part * rows, rows)
@@ -706,16 +762,18 @@
             flush(sum_buffer, sums)
         load(4 * b).wait()
         for part in range(parts):
-            grad_buffer[:, :, part * rows : (part + 1) * rows] = grads_in[part][..., :rows]
+            for at in range(size):
+                grad_buffer[at, :, part * rows : (part + 1) * rows] = whole(grads_in[part, at])
         flush(grad_buffer, grads)
     for copy in pending:
         copy.wait()
 
 
-def finish(roomy, results, rows_of, scale):
+def finish(roomy, results, sizes, rows_of, scale):
     outs, buffers = [], []
     for b in range(2):
-        parts, size, tokens, _ = results[4 * b].shape
+        parts = results[4 * b].shape[0]
+        size, tokens = sizes
         rows = rows_of[b]
         shapes = [((size, tokens, parts * rows), jnp.bfloat16), ((rows, parts * rows), jnp.float32)]
         outs += [jax.ShapeDtypeStruct(*shape) for shape in shapes]
@@ -745,7 +803,7 @@
         [t5_top_grad, vit_top_grad],
     )
     t5_grads, t5_sum, vit_grads, vit_sum = finish(
-        roomy, results, [t5_weight.shape[1], vit_weight.shape[1]], scale
+        roomy, results, (size, tokens), [t5_weight.shape[1], vit_weight.shape[1]], scale
     )
     return vit_grads[None], t5_grads[None], vit_sum[None], t5_sum[None]
 

time: 129 us -> 123 us (0.953)
  Pallas kernels: 128 us -> 122 us
    pallas_call x1, Pallas kernels: 123 us -> 116 us  [branch_call(): pl.pallas_call(functools.partial(kernel, sections, parts, size, roomy, sc...]
where the time goes in v2:
time: 123 us
  Pallas kernels  122 us (99%)
    pallas_call x1, Pallas kernels, branch_call(): pl.pallas_call(functools.partial(kernel, sections, parts, size, roomy, sc...  116 us
    pallas_call x1, Pallas kernels, finish(): pl.pallas_call(functools.partial(finish_kernel, roomy, scale), out_shape=...  5.65 us

profile of v2, /device:TPU:0, one launch (start us, length us, event | category | flops | bytes accessed | tf_op | source)
XLA Modules:
  0.0 122.6 jit_solution(11846185225056099641)
XLA Ops:
  0.6 116.3 %shard_map.93 = (bf16[4,4,32,512]{3,2,1,0:T(8,128)(2,1)}, bf16[1,4,32,512]{3,2,1,0:T(8,128)(2,1)}, bf16[4,4,32,512]{3,2,1,0:T(8,128)(2,1)}, f32[4,512,512]{2,1,0...) custom-call(bf16[512,2048]{1,0:T(8,128)(2,1)} %bitcast.8, ...), custom_call_target="tpu_custom_call" | custom-call | tf_op jit(solution)/shard_map/pallas_call | solution.py:694
  116.9 5.7 %shard_map.94 = (bf16[4,32,2048]{2,1,0:T(8,128)(2,1)}, f32[512,2048]{1,0:T(8,128)}, bf16[4,32,1280]{2,1,0:T(8,128)(2,1)}, f32[320,1280]{1,0:T(8,128)}) custom-call(bf16[4,4,32,512]{3,2,1,0:T(8,128)(2,1)} %get-tuple-element.16.refs_0_, bf16[1,4,32,512]{3,2,1,0:T(8,128)(2,1)} %get-tuple-element.17.refs_1_, bf16[4,4,32,512]{3,2,1,0:T(8,128)(2,1)} %get-tuple-element.18.refs_2_, ...), custom_call_target="tpu_custom_call" | custom-call | tf_op jit(solution)/shard_map/pallas_call | solution.py:781

commit v3 on v2

--- a/solution.py
+++ b/solution.py
@@ -23,6 +23,7 @@
     "pair_out", "pair_in", "chip_in", "slopes", "sums", "saved_got", "above_got", "pair_got",
     "chip_got", "near_got", "far_got", "slope_got", "out_got", "sent", "top_sent", "top_got",
     "lift_sent",
+    "weight_raw", "top_raw", "raw_got",
 )
 SENDS = ("saved", "pair", "chip", "near", "far", "slope", "hop", "out", "columns", "local", "sums")
 
@@ -133,6 +134,17 @@
         for group in range(parts):
             groups[group] = padded(source[..., group * cut : (group + 1) * cut], groups.shape[-1])
 
+    def weight_load(br):
+        return pltpu.make_async_copy(br.weight_in, br.weight_raw, br.raw_got.at[0])
+
+    def top_load(br):
+        return pltpu.make_async_copy(br.top_in, br.top_raw, br.raw_got.at[1])
+
+    for br in branches:
+        top_load(br).start()
+    for br in branches:
+        weight_load(br).start()
+
     barrier = pltpu.get_barrier_semaphore()
     for k in range(1, parts):
         pl.semaphore_signal(barrier, inc=1, device_id=(section, lax.rem(me + k, parts)), device_id_type=MESH)
@@ -154,9 +166,11 @@
     with jax.named_scope("regroup_saved"):
         for br in branches:
             regroup(br.saved_in, br.saved)
+        for br in branches:
+            top_load(br).wait()
             for group in range(parts):
                 for at in range(size):
-                    block = br.top_in[at, :, group * br.rows : (group + 1) * br.rows]
+                    block = br.top_raw[at, :, group * br.rows : (group + 1) * br.rows]
                     br.top[group, at] = packed(br, block.astype(jnp.float32)).astype(jnp.bfloat16)
     greeted = parts * lax.min(section, 1) + lax.min(last - section, 1)
     with jax.named_scope("barrier"):
@@ -212,7 +226,7 @@
         return copy(br.saved.at[to, span], br.columns.at[0, span], sent(br, "saved"), br.saved_got.at[h * parts], section, to)
 
     def piecewise(turn):
-        return jnp.logical_and(is_last, turn == chips)
+        return jnp.logical_and(is_last, turn >= chips)
 
     def piece_copy(br, m, k):
         to, turn, at = lax.rem(me + k, parts), m // size, lax.rem(m, size)
@@ -240,6 +254,10 @@
                         for br in branches:
                             for k in range(1, parts):
                                 half_copy(br, h, k).start()
+
+                @pl.when(turn > chips)
+                def _():
+                    pl.loop(0, first_size)(lambda at: send_piece(turn * size + at))
 
                 @pl.when(jnp.logical_and(turn > 0, jnp.logical_not(piecewise(turn))))
                 def _():
@@ -417,7 +435,8 @@
                 )
                 left, right = left[:, : br.rows], right[:, : br.rows]
                 term = lax.dot_general(left, right, (((0,), (0,)), ((), ())), preferred_element_type=jnp.float32)
-                br.sums[group] = br.sums[group] + (term * scale).astype(jnp.bfloat16).astype(jnp.float32)
+                total = br.sums[group] + (term * scale).astype(jnp.bfloat16).astype(jnp.float32)
+                br.sums[group] = total
 
                 @pl.when(turn == parts - 2)
                 def _():
@@ -441,8 +460,9 @@
         for br in branches:
             rows = br.weight_in.shape[0]
             wide = br.weight.shape[-1]
+            weight_load(br).wait()
             for group in range(parts):
-                block = padded(br.weight_in[:, group * rows : (group + 1) * rows], wide)
+                block = padded(br.weight_raw[:, group * rows : (group + 1) * rows], wide)
                 br.weight[group, :rows] = block
                 if wide > rows:
                     br.weight[group, rows:] = jnp.zeros((wide - rows, wide), block.dtype)
@@ -475,6 +495,10 @@
     def _(at):
         send_piece(at + chips * size)
 
+    @pl.loop(chips + 1, parts)
+    def _(turn):
+        pl.loop(first_size, size)(lambda at: send_piece(turn * size + at))
+
     @pl.when(jnp.logical_not(is_last))
     def _():
         lift(early, count)
@@ -558,7 +582,7 @@
             def _():
                 hand_out(m)
 
-            @pl.when(jnp.logical_and(section == 1, m >= size))
+            @pl.when(jnp.logical_and(section == 1, jnp.logical_and(m >= size, m < count - size)))
             def _():
                 hand_out(mixed(lax.max(m - size, 0)))
 
@@ -568,7 +592,7 @@
 
         @pl.when(section == 1)
         def _():
-            pl.loop(count - size, count)(lambda i: hand_out(mixed(i)))
+            pl.loop(max(count - 2 * size, 0), count)(lambda i: hand_out(mixed(i)))
 
         @pl.when(section > 1)
         def _():
@@ -690,11 +714,14 @@
             dma((turns,)),
             dma((turns,)),
             dma((turns,)),
+            pltpu.VMEM(weight.shape, half),
+            pltpu.VMEM(top.shape, half),
+            dma((2,)),
         ]
     return roomy, pl.pallas_call(
         functools.partial(kernel, sections, parts, size, roomy, scale),
         out_shape=outs,
-        in_specs=[vmem] * len(operands),
+        in_specs=[anywhere, vmem, anywhere] * 2,
         out_specs=out_specs,
         scratch_shapes=scratch,
         compiler_params=pltpu.CompilerParams(

time: 123 us -> 122 us (level)
  no operation moved by 1% of the time
where the time goes in v3:
time: 122 us
  Pallas kernels  121 us (99%)
    pallas_call x1, Pallas kernels, branch_call(): pl.pallas_call(functools.partial(kernel, sections, parts, size, roomy, sc...  115 us
    pallas_call x1, Pallas kernels, finish(): pl.pallas_call(functools.partial(finish_kernel, roomy, scale), out_shape=...  5.65 us

profile of v3, /device:TPU:0, one launch (start us, length us, event | category | flops | bytes accessed | tf_op | source)
XLA Modules:
  0.0 121.6 jit_solution(776968260760859754)
XLA Ops:
  0.6 115.3 %shard_map.93 = (bf16[4,4,32,512]{3,2,1,0:T(8,128)(2,1)}, bf16[1,4,32,512]{3,2,1,0:T(8,128)(2,1)}, bf16[4,4,32,512]{3,2,1,0:T(8,128)(2,1)}, f32[4,512,512]{2,1,0...) custom-call(bf16[512,2048]{1,0:T(8,128)(2,1)} %bitcast.8, ...), custom_call_target="tpu_custom_call" | custom-call | tf_op jit(solution)/shard_map/pallas_call | solution.py:721
  116.0 5.7 %shard_map.94 = (bf16[4,32,2048]{2,1,0:T(8,128)(2,1)}, f32[512,2048]{1,0:T(8,128)}, bf16[4,32,1280]{2,1,0:T(8,128)(2,1)}, f32[320,1280]{1,0:T(8,128)}) custom-call(bf16[4,4,32,512]{3,2,1,0:T(8,128)(2,1)} %get-tuple-element.16.refs_0_, bf16[1,4,32,512]{3,2,1,0:T(8,128)(2,1)} %get-tuple-element.17.refs_1_, bf16[4,4,32,512]{3,2,1,0:T(8,128)(2,1)} %get-tuple-element.18.refs_2_, ...), custom_call_target="tpu_custom_call" | custom-call | tf_op jit(solution)/shard_map/pallas_call | solution.py:808

commit v4 on v3

--- a/solution.py
+++ b/solution.py
@@ -191,8 +191,11 @@
         turn = m // sections
         return copy(br.lifted.at[turn], br.above.at[m, slot(me)], br.lift_sent.at[turn], br.above_got.at[m], last, me)
 
+    def batch(m):
+        return lax.min(m, size + lax.max(m // size - 1, 0))
+
     def pair_copy(br, m):
-        return copy(br.pair_out.at[m], br.pair_in.at[m], sent(br, "pair"), br.pair_got.at[m], section, partner)
+        return copy(br.pair_out.at[m], br.pair_in.at[m], sent(br, "pair"), br.pair_got.at[batch(m)], section, partner)
 
     def chip_copy(br, m, k):
         return copy(br.mine.at[m, k], br.chip_in.at[m, k - 1], sent(br, "chip"), br.chip_got.at[m], section, ahead(k))
@@ -216,7 +219,7 @@
 
     def slope_near(br, m, k):
         group = behind(k)
-        return copy(br.slopes.at[m, group], br.slopes.at[m, group], sent(br, "slope"), br.slope_got.at[m], section, partner)
+        return copy(br.slopes.at[m, group], br.slopes.at[m, group], sent(br, "slope"), br.slope_got.at[m // size], section, partner)
 
     def out_copy(br, m):
         return copy(br.below.at[m], br.out.at[me, lax.rem(m, size)], sent(br, "out"), br.out_got.at[0], section, owner(m))
@@ -323,7 +326,14 @@
 
     def pair_sum(m):
         for br in branches:
-            drain(br.pair_in.at[m], br.pair_got.at[m])
+            @pl.when(m < size)
+            def _():
+                drain(br.pair_in.at[m], br.pair_got.at[batch(m)])
+
+            @pl.when(jnp.logical_and(m >= size, lax.rem(m, size) == 0))
+            def _():
+                drain(br.pair_in.at[pl.ds(0, size)], br.pair_got.at[batch(m)])
+
             for k in range(1, chips):
                 both = br.mine[m, k].astype(jnp.float32) + br.pair_in[m, k].astype(jnp.float32)
                 br.mine[m, k] = both.astype(jnp.bfloat16)
@@ -398,7 +408,10 @@
     @jax.named_scope("descend_wide")
     def descend_wide(m):
         for br in branches:
-            drain(br.local.at[m, pl.ds(0, chips)], br.slope_got.at[m])
+            @pl.when(lax.rem(m, size) == 0)
+            def _():
+                drain(br.local.at[pl.ds(0, size), pl.ds(0, chips)], br.slope_got.at[m // size])
+
             drain(br.local.at[m, pl.ds(0, chips)], br.near_got.at[m])
             blocks = []
             for group in range(parts):
@@ -704,11 +717,11 @@
             pltpu.VMEM(all_sums, full),
             dma((parts + 1,)),
             dma((count,)),
+            dma((size + parts,)),
             dma((count,)),
             dma((count,)),
             dma((count,)),
-            dma((count,)),
-            dma((count if roomy else 1,)),
+            dma((parts,)),
             dma((1,)),
             dma((len(SENDS),)),
             dma((turns,)),

time: 122 us -> 121 us (level)
  no operation moved by 1% of the time
where the time goes in v4:
time: 121 us
  Pallas kernels  121 us (100%)
    pallas_call x1, Pallas kernels, branch_call(): pl.pallas_call(functools.partial(kernel, sections, parts, size, roomy, sc...  115 us
    pallas_call x1, Pallas kernels, finish(): pl.pallas_call(functools.partial(finish_kernel, roomy, scale), out_shape=...  5.66 us

profile of v4, /device:TPU:0, one launch (start us, length us, event | category | flops | bytes accessed | tf_op | source)
XLA Modules:
  0.0 121.3 jit_solution(14305430416706401416)
XLA Ops:
  0.6 115.0 %shard_map.93 = (bf16[4,4,32,512]{3,2,1,0:T(8,128)(2,1)}, bf16[1,4,32,512]{3,2,1,0:T(8,128)(2,1)}, bf16[4,4,32,512]{3,2,1,0:T(8,128)(2,1)}, f32[4,512,512]{2,1,0...) custom-call(bf16[512,2048]{1,0:T(8,128)(2,1)} %bitcast.8, ...), custom_call_target="tpu_custom_call" | custom-call | tf_op jit(solution)/shard_map/pallas_call | solution.py:734
  115.7 5.7 %shard_map.94 = (bf16[4,32,2048]{2,1,0:T(8,128)(2,1)}, f32[512,2048]{1,0:T(8,128)}, bf16[4,32,1280]{2,1,0:T(8,128)(2,1)}, f32[320,1280]{1,0:T(8,128)}) custom-call(bf16[4,4,32,512]{3,2,1,0:T(8,128)(2,1)} %get-tuple-element.16.refs_0_, bf16[1,4,32,512]{3,2,1,0:T(8,128)(2,1)} %get-tuple-element.17.refs_1_, bf16[4,4,32,512]{3,2,1,0:T(8,128)(2,1)} %get-tuple-element.18.refs_2_, ...), custom_call_target="tpu_custom_call" | custom-call | tf_op jit(solution)/shard_map/pallas_call | solution.py:821
